TPU v7x, 32 devices: a whole 2x2x4 slice. The times are simulated.
32 devices in a mesh: dp: 4 (over y, x), seq: 8 (over z, core).
Axes of the slice: x: 2, y: 2, z: 4, core: 2. Of those that a mesh axis runs over, the one named last changes fastest.
Arguments:
- layer_input: bfloat16 [2, 4, 1024, 1600], P(None, 'dp', 'seq'), may hold values from -3 to 3
- cotangent: bfloat16 [2, 4, 1024, 1600], P(None, 'dp', 'seq'), may hold values from -1.5 to 1.5
- block_order: int32 [16], replicated, may hold values from 0 to 15, as said below
- w_qkv: bfloat16 [1600, 4800], P('dp', 'seq'), may hold values from -0.15625 to 0.15625
- w_out: bfloat16 [1600, 1600], P('dp', 'seq'), may hold values from -1.75 to 1.75
- w_up: bfloat16 [1600, 6400], P('dp', 'seq'), may hold values from -0.15625 to 0.15625
- w_down: bfloat16 [6400, 1600], P('dp', 'seq'), may hold values from -0.078125 to 0.078125
- vectors: bfloat16 [12, 1600], P('dp', 'seq'), may hold values from -2 to 2
Outputs:
- output: bfloat16 [2, 4, 1024, 1600], P(None, 'dp', 'seq')
- grad_input: bfloat16 [2, 4, 1024, 1600], P(None, 'dp', 'seq')
- grad_w_qkv: float32 [1600, 4800], P('dp', 'seq')
- grad_w_out: float32 [1600, 1600], P('dp', 'seq')
- grad_w_up: float32 [1600, 6400], P('dp', 'seq')
- grad_w_down: float32 [6400, 1600], P('dp', 'seq')
- grad_vectors: float32 [12, 1600], P('dp', 'seq')
Inputs may be any that keep to these rules, and one draw needn't show every extreme that they name: block_order holds every block number once; its entries 2i and 2i + 1 sum to 15, and entry 2i is below 8.
All inputs are finite; a program needn't handle non-finite values.
Results may differ from a plain program's by a relative error of at most 0.018.
Values may be sent and summed in bfloat16 or wider, within the bound.
A program may use at most 448 MiB of HBM per device.

v0:
```python
import jax
import jax.numpy as jnp
from jax import lax
from jax.sharding import PartitionSpec as P

D = 1600
FF = 6400
HEADS = 25
HEAD_DIM = 64


EPSILON = 1e-05
SCALE = 0.125
CUBIC = 0.044715
ROOT_TWO_PI = 0.7978845608028654


def gelu_tanh(values):
    return (
        0.5 * values * (1.0 + jnp.tanh(ROOT_TWO_PI * (values + CUBIC * values * values * values)))
    )


def norm_forward(values, gain, shift):
    center = values - jnp.mean(values, axis=-1, keepdims=True)
    scale = lax.rsqrt(jnp.mean(center * center, axis=-1, keepdims=True) + EPSILON)
    normed = center * scale
    return (normed * gain + shift, normed, scale)


def norm_backward(grad_out, normed, scale, gain):
    scaled = grad_out * gain
    first = jnp.mean(scaled, axis=-1, keepdims=True)
    second = jnp.mean(scaled * normed, axis=-1, keepdims=True)
    return (
        scale * (scaled - first - normed * second),
        jnp.sum(grad_out * normed, axis=0),
        jnp.sum(grad_out, axis=0),
    )


def across_rows(left, right):
    return lax.dot_general(
        left, right, (((0,), (0,)), ((), ())), preferred_element_type=jnp.float32
    )


def across_columns(left, right):
    return lax.dot_general(
        left, right, (((1,), (1,)), ((), ())), preferred_element_type=jnp.float32
    )


def positions(block_order, first, count, block):
    token_ids = first + jnp.arange(count, dtype=jnp.int32)
    slots = token_ids // block
    hits = slots[:, None] == jnp.arange(block_order.shape[0], dtype=jnp.int32)[None, :]
    owner = jnp.sum(jnp.where(hits, block_order[None, :], 0), axis=1)
    return owner * block + token_ids % block


def head_group():
    for width in (5, 4, 3, 2, 1):
        return width
    return 1


def fetch(w_qkv, w_out, w_up, w_down, vectors):
    rows = (
        lax.all_gather(w_qkv, "dp", axis=0, tiled=True),
        lax.all_gather(w_out, "dp", axis=0, tiled=True),
        lax.all_gather(w_up, "dp", axis=0, tiled=True),
        lax.all_gather(w_down, "dp", axis=0, tiled=True),
        lax.all_gather(vectors, "dp", axis=0, tiled=True),
    )
    return (
        lax.all_gather(rows[0], "seq", axis=1, tiled=True),
        lax.all_gather(rows[1], "seq", axis=1, tiled=True),
        lax.all_gather(rows[2], "seq", axis=1, tiled=True),
        lax.all_gather(rows[3], "seq", axis=1, tiled=True),
        lax.all_gather(rows[4], "seq", axis=1, tiled=True),
    )


def attend(queries, keys_all, values_all, allowed):
    rows = queries.shape[0]
    total = keys_all.shape[0]
    width = head_group()
    span = width * HEAD_DIM

    def group(index, carry):
        mixed, logsum = carry
        start = index * span
        query_part = lax.dynamic_slice_in_dim(queries, start, span, 1).reshape(
            rows, width, HEAD_DIM
        )
        key_part = lax.dynamic_slice_in_dim(keys_all, start, span, 1).reshape(
            total, width, HEAD_DIM
        )
        value_part = lax.dynamic_slice_in_dim(values_all, start, span, 1).reshape(
            total, width, HEAD_DIM
        )
        scores = (
            jnp.einsum("qhd,khd->hqk", query_part, key_part, preferred_element_type=jnp.float32)
            * SCALE
        )
        scores = jnp.where(allowed[None], scores, -1e30)
        peak = jnp.max(scores, axis=-1, keepdims=True)
        raised = jnp.exp(scores - peak)
        summed = jnp.sum(raised, axis=-1, keepdims=True)
        weights = (raised / summed).astype(jnp.bfloat16)
        part = jnp.einsum("hqk,khd->qhd", weights, value_part, preferred_element_type=jnp.float32)
        mixed = lax.dynamic_update_slice_in_dim(mixed, part.reshape(rows, span), start, 1)
        logsum = lax.dynamic_update_slice_in_dim(
            logsum, (peak + jnp.log(summed))[..., 0], index * width, 0
        )
        return (mixed, logsum)

    empty = (
        jnp.zeros((rows, HEADS * HEAD_DIM), jnp.float32),
        jnp.zeros((HEADS, rows), jnp.float32),
    )
    return lax.fori_loop(0, HEADS // width, group, empty)


def score_terms(query_part, key_part, value_part, grad_part, level, allowed):
    scores = (
        jnp.einsum("qhd,khd->hqk", query_part, key_part, preferred_element_type=jnp.float32) * SCALE
    )
    scores = jnp.where(allowed[None], scores, -1e30)
    weights = jnp.exp(scores - level[..., None])
    grad_weights = jnp.einsum(
        "qhd,khd->hqk", grad_part, value_part, preferred_element_type=jnp.float32
    )
    offset = jnp.sum(weights * grad_weights, axis=-1, keepdims=True)
    grad_scores = weights * (grad_weights - offset)
    return (weights.astype(jnp.bfloat16), grad_scores.astype(jnp.bfloat16))


def attend_back(queries, keys_all, values_all, grad_mixed, logsum, allowed):
    rows = queries.shape[0]
    total = keys_all.shape[0]
    width = head_group()
    span = width * HEAD_DIM

    def group(index, carry):
        grad_query, grad_keys, grad_values = carry
        start = index * span
        query_part = lax.dynamic_slice_in_dim(queries, start, span, 1).reshape(
            rows, width, HEAD_DIM
        )
        key_part = lax.dynamic_slice_in_dim(keys_all, start, span, 1).reshape(
            total, width, HEAD_DIM
        )
        value_part = lax.dynamic_slice_in_dim(values_all, start, span, 1).reshape(
            total, width, HEAD_DIM
        )
        grad_part = lax.dynamic_slice_in_dim(grad_mixed, start, span, 1).reshape(
            rows, width, HEAD_DIM
        )
        level = lax.dynamic_slice_in_dim(logsum, index * width, width, 0)
        rounded, grad_rounded = score_terms(
            query_part, key_part, value_part, grad_part, level, allowed
        )
        values_term = jnp.einsum(
            "hqk,qhd->khd", rounded, grad_part, preferred_element_type=jnp.float32
        )
        query_term = (
            jnp.einsum("hqk,khd->qhd", grad_rounded, key_part, preferred_element_type=jnp.float32)
            * SCALE
        )
        keys_term = (
            jnp.einsum("hqk,qhd->khd", grad_rounded, query_part, preferred_element_type=jnp.float32)
            * SCALE
        )
        grad_query = lax.dynamic_update_slice_in_dim(
            grad_query, query_term.reshape(rows, span), start, 1
        )
        grad_keys = lax.dynamic_update_slice_in_dim(
            grad_keys, keys_term.reshape(total, span), start, 1
        )
        grad_values = lax.dynamic_update_slice_in_dim(
            grad_values, values_term.reshape(total, span), start, 1
        )
        return (grad_query, grad_keys, grad_values)

    empty = (
        jnp.zeros((rows, HEADS * HEAD_DIM), jnp.float32),
        jnp.zeros((total, HEADS * HEAD_DIM), jnp.float32),
        jnp.zeros((total, HEADS * HEAD_DIM), jnp.float32),
    )
    return lax.fori_loop(0, HEADS // width, group, empty)


def forward_block(full, tokens, allowed):
    w_qkv, w_out, w_up, w_down, vectors = full
    table = vectors.astype(jnp.float32)
    width = tokens.shape[1]
    residual = tokens.astype(jnp.float32)
    normed_one, first_norm, first_scale = norm_forward(residual, table[0], table[1])
    entry_one = normed_one.astype(jnp.bfloat16)
    joined = jnp.dot(entry_one, w_qkv, preferred_element_type=jnp.float32)
    queries = (joined[:, :width] + table[4]).astype(jnp.bfloat16)
    keys_own = joined[:, width : 2 * width].astype(jnp.bfloat16)
    values_own = (joined[:, 2 * width :] + table[5]).astype(jnp.bfloat16)
    keys_all, values_all = (
        lax.all_gather(keys_own, "seq", axis=0, tiled=True),
        lax.all_gather(values_own, "seq", axis=0, tiled=True),
    )
    mixed, logsum = attend(queries, keys_all, values_all, allowed)
    mixed_low = mixed.astype(jnp.bfloat16)
    middle = residual + jnp.dot(mixed_low, w_out, preferred_element_type=jnp.float32) + table[6]
    normed_two, second_norm, second_scale = norm_forward(middle, table[2], table[3])
    entry_two = normed_two.astype(jnp.bfloat16)
    hidden_pre = jnp.dot(entry_two, w_up, preferred_element_type=jnp.float32) + table[8:].reshape(
        -1
    )
    hidden = gelu_tanh(hidden_pre).astype(jnp.bfloat16)
    result = (
        middle + jnp.dot(hidden, w_down, preferred_element_type=jnp.float32) + table[7]
    ).astype(jnp.bfloat16)
    kept = (
        queries,
        keys_own,
        values_own,
        logsum,
        mixed_low,
        mixed,
        first_norm,
        first_scale,
        entry_one,
        second_norm,
        second_scale,
        entry_two,
        hidden_pre,
        hidden,
    )
    return (result, kept)


def backward_block(full, kept, grad_out, allowed):
    w_qkv, w_out, w_up, w_down, vectors = full
    table = vectors.astype(jnp.float32)
    (
        queries,
        keys_own,
        values_own,
        logsum,
        mixed_low,
        mixed_wide,
        first_norm,
        first_scale,
        entry_one,
        second_norm,
        second_scale,
        entry_two,
        hidden_pre,
        hidden,
    ) = kept
    width = queries.shape[1]
    grad_top = grad_out.astype(jnp.float32)
    grad_w_down = across_rows(hidden, grad_out)
    grad_hidden = across_columns(grad_out, w_down)
    ignored, pull = jax.vjp(gelu_tanh, hidden_pre)
    grad_pre = pull(grad_hidden)[0].astype(jnp.bfloat16)
    grad_w_up = across_rows(entry_two, grad_pre)
    grad_entry_two = across_columns(grad_pre, w_up)
    grad_middle, grad_gain_two, grad_shift_two = norm_backward(
        grad_entry_two, second_norm, second_scale, table[2]
    )
    grad_middle = grad_middle + grad_top
    grad_branch = grad_middle.astype(jnp.bfloat16)
    grad_w_out = across_rows(mixed_low, grad_branch)
    grad_mixed = across_columns(grad_branch, w_out).astype(jnp.bfloat16)
    keys_all, values_all = (
        lax.all_gather(keys_own, "seq", axis=0, tiled=True),
        lax.all_gather(values_own, "seq", axis=0, tiled=True),
    )
    grad_query, grad_keys, grad_values = attend_back(
        queries, keys_all, values_all, grad_mixed, logsum, allowed
    )
    grad_key_own, grad_value_own = (
        lax.psum_scatter(
            grad_keys.astype(jnp.bfloat16), "seq", scatter_dimension=0, tiled=True
        ).astype(jnp.float32),
        lax.psum_scatter(
            grad_values.astype(jnp.bfloat16), "seq", scatter_dimension=0, tiled=True
        ).astype(jnp.float32),
    )
    grad_joined = jnp.concatenate(
        [
            grad_query.astype(jnp.bfloat16),
            grad_key_own.astype(jnp.bfloat16),
            grad_value_own.astype(jnp.bfloat16),
        ],
        axis=1,
    )
    grad_w_qkv = across_rows(entry_one, grad_joined)
    grad_entry_one = across_columns(grad_joined, w_qkv)
    grad_residual, grad_gain_one, grad_shift_one = norm_backward(
        grad_entry_one, first_norm, first_scale, table[0]
    )
    joined_wide = grad_joined.astype(jnp.float32)
    small_rows = jnp.stack(
        [
            grad_gain_one,
            grad_shift_one,
            grad_gain_two,
            grad_shift_two,
            jnp.sum(joined_wide[:, :width], axis=0),
            jnp.sum(joined_wide[:, 2 * width :], axis=0),
            jnp.sum(grad_branch.astype(jnp.float32), axis=0),
            jnp.sum(grad_top, axis=0),
        ]
    )
    up_rows = jnp.sum(grad_pre.astype(jnp.float32), axis=0).reshape(4, width)
    grad_vectors = jnp.concatenate([small_rows, up_rows], axis=0)
    grad_input = (grad_residual + grad_middle).astype(jnp.bfloat16)
    return ((grad_w_qkv, grad_w_out, grad_w_up, grad_w_down, grad_vectors), grad_input)


def shards(layer_input, cotangent, block_order, w_qkv, w_out, w_up, w_down, vectors):
    per_seq = layer_input.shape[2]
    block = per_seq // 2
    length = per_seq * lax.axis_size("seq")
    own_positions = positions(block_order, lax.axis_index("seq") * per_seq, per_seq, block)
    key_positions = positions(block_order, 0, length, block)
    allowed = key_positions[None, :] <= own_positions[:, None]
    inputs = layer_input[:, 0]
    grads_in = cotangent[:, 0]

    def forward_weights():
        return fetch(w_qkv, w_out, w_up, w_down, vectors)

    def forward_step(carry, tokens):
        result, kept = forward_block(forward_weights(), tokens, allowed)
        return (carry, (result, kept))

    ignored, (outputs, kept_all) = lax.scan(forward_step, jnp.zeros((), jnp.float32), inputs)

    def backward_weights():
        return fetch(w_qkv, w_out, w_up, w_down, vectors)

    def backward_step(totals, item):
        kept, grad_out = item
        grads, grad_input = backward_block(backward_weights(), kept, grad_out, allowed)
        return (tuple((left + right for left, right in zip(totals, grads))), grad_input)

    zeros = (
        jnp.zeros((D, 3 * D), jnp.float32),
        jnp.zeros((D, D), jnp.float32),
        jnp.zeros((D, FF), jnp.float32),
        jnp.zeros((FF, D), jnp.float32),
        jnp.zeros((12, D), jnp.float32),
    )
    totals, grad_inputs = lax.scan(backward_step, zeros, (kept_all, grads_in))
    columns = (
        lax.psum_scatter(
            totals[0].astype(jnp.bfloat16), "seq", scatter_dimension=1, tiled=True
        ).astype(jnp.float32),
        lax.psum_scatter(
            totals[1].astype(jnp.bfloat16), "seq", scatter_dimension=1, tiled=True
        ).astype(jnp.float32),
        lax.psum_scatter(
            totals[2].astype(jnp.bfloat16), "seq", scatter_dimension=1, tiled=True
        ).astype(jnp.float32),
        lax.psum_scatter(
            totals[3].astype(jnp.bfloat16), "seq", scatter_dimension=1, tiled=True
        ).astype(jnp.float32),
        lax.psum_scatter(
            totals[4].astype(jnp.bfloat16), "seq", scatter_dimension=1, tiled=True
        ).astype(jnp.float32),
    )
    owned = (
        lax.psum_scatter(
            columns[0].astype(jnp.bfloat16), "dp", scatter_dimension=0, tiled=True
        ).astype(jnp.float32),
        lax.psum_scatter(
            columns[1].astype(jnp.bfloat16), "dp", scatter_dimension=0, tiled=True
        ).astype(jnp.float32),
        lax.psum_scatter(
            columns[2].astype(jnp.bfloat16), "dp", scatter_dimension=0, tiled=True
        ).astype(jnp.float32),
        lax.psum_scatter(
            columns[3].astype(jnp.bfloat16), "dp", scatter_dimension=0, tiled=True
        ).astype(jnp.float32),
        lax.psum_scatter(
            columns[4].astype(jnp.bfloat16), "dp", scatter_dimension=0, tiled=True
        ).astype(jnp.float32),
    )
    return (
        outputs[:, None],
        grad_inputs[:, None],
        owned[0],
        owned[1],
        owned[2],
        owned[3],
        owned[4],
    )


def solution(mesh):
    in_specs = (
        P(None, "dp", "seq", None),
        P(None, "dp", "seq", None),
        P(),
        P("dp", "seq"),
        P("dp", "seq"),
        P("dp", "seq"),
        P("dp", "seq"),
        P("dp", "seq"),
    )
    out_specs = (
        P(None, "dp", "seq", None),
        P(None, "dp", "seq", None),
        P("dp", "seq"),
        P("dp", "seq"),
        P("dp", "seq"),
        P("dp", "seq"),
        P("dp", "seq"),
    )
    return jax.shard_map(shards, mesh=mesh, in_specs=in_specs, out_specs=out_specs, check_vma=False)
```

profile of v0, /device:TPU:0, one launch (start us, length us, event | category | flops | bytes accessed | tf_op | source)
XLA Modules:
  0.0 4480.8 jit_solution(18022377539014405624)
XLA Ops:
  17.4 1588.9 %while.93 = (s32[]{:T(128)}, bf16[2,128,1600]{1,2,0:T(8,128)(2,1)}, bf16[2,128,1600]{1,2,0:T(8,128)(2,1)}, bf16[2,128,1600]{1,2,0:T(8,128)(2,1)}, bf16[2,128,160...) while((s32[]{:T(128)}, bf16[2,128,1600]{1,2,0:T(8,128)(2,1)}, ...), condition=%wide.region_11.12_spmd.clone, body=%wide.region_2.11_spmd.clone.sunk | while | flops 8065296384 | bytes 415582880 | solution.py:339
  90.7 116.1 %all-gather.55.cloned.1.call-done = bf16[1600,4800]{0,1:T(8,128)(2,1)} async-done(((bf16[1600,600]{0,1:T(8,128)(2,1)}), bf16[1600,4800]{0,1:T(8,128)(2,1)}) %all-gather.55.cloned.1.call-update) | async-done | bytes 15360016 | tf_op jit(solution)/shard_map/while/body/eval_jaxpr/all_gather | solution.py:77
  440.8 180.7 %all-gather.67.cloned.1.call-done = bf16[1600,6400]{0,1:T(8,128)(2,1)} async-done(((bf16[1600,800]{0,1:T(8,128)(2,1)}), bf16[1600,6400]{0,1:T(8,128)(2,1)}) %all-gather.67.cloned.1.call-update) | async-done | bytes 20480016 | tf_op jit(solution)/shard_map/while/body/eval_jaxpr/all_gather | solution.py:79
  639.5 163.3 %all-gather.63.cloned.1.call-done = bf16[6400,1600]{0,1:T(8,128)(2,1)} async-done(((bf16[6400,200]{0,1:T(8,128)(2,1)}), bf16[6400,1600]{0,1:T(8,128)(2,1)}) %all-gather.63.cloned.1.call-update) | async-done | bytes 20480016 | tf_op jit(solution)/shard_map/while/body/eval_jaxpr/all_gather | solution.py:80
  883.1 116.1 %all-gather.55.cloned.1.call-done = bf16[1600,4800]{0,1:T(8,128)(2,1)} async-done(((bf16[1600,600]{0,1:T(8,128)(2,1)}), bf16[1600,4800]{0,1:T(8,128)(2,1)}) %all-gather.55.cloned.1.call-update) | async-done | bytes 15360016 | tf_op jit(solution)/shard_map/while/body/eval_jaxpr/all_gather | solution.py:77
  1127.5 40.5 all-gather.59.cloned.1.call-done
  1232.9 180.5 %all-gather.67.cloned.1.call-done = bf16[1600,6400]{0,1:T(8,128)(2,1)} async-done(((bf16[1600,800]{0,1:T(8,128)(2,1)}), bf16[1600,6400]{0,1:T(8,128)(2,1)}) %all-gather.67.cloned.1.call-update) | async-done | bytes 20480016 | tf_op jit(solution)/shard_map/while/body/eval_jaxpr/all_gather | solution.py:79
  1431.3 163.2 %all-gather.63.cloned.1.call-done = bf16[6400,1600]{0,1:T(8,128)(2,1)} async-done(((bf16[6400,200]{0,1:T(8,128)(2,1)}), bf16[6400,1600]{0,1:T(8,128)(2,1)}) %all-gather.63.cloned.1.call-update) | async-done | bytes 20480016 | tf_op jit(solution)/shard_map/while/body/eval_jaxpr/all_gather | solution.py:80
  1607.4 1855.1 %while.95 = (s32[]{:T(128)}, f32[1600,4800]{1,0:T(8,128)}, f32[1600,1600]{1,0:T(8,128)}, f32[1600,6400]{1,0:T(8,128)}, f32[6400,1600]{0,1:T(8,128)}, /*index=5*/...) while((s32[]{:T(128)}, f32[1600,4800]{1,0:T(8,128)}, ...), condition=%wide.region_31.32_spmd.clone, body=%wide.region_12.31_spmd.clone.sunk | while | flops 16256249856 | bytes 751455872 | solution.py:356
  1768.4 129.9 %all-gather.75.cloned.1.call-done = bf16[6400,1600]{0,1:T(8,128)(2,1)} async-done(((bf16[6400,200]{0,1:T(8,128)(2,1)}), bf16[6400,1600]{0,1:T(8,128)(2,1)}) %all-gather.75.cloned.1.call-update) | async-done | bytes 20480016 | tf_op jit(solution)/shard_map/while/body/eval_jaxpr/all_gather | solution.py:80
  1910.3 176.1 %all-gather.79.cloned.1.call-done = bf16[1600,6400]{0,1:T(8,128)(2,1)} async-done(((bf16[1600,800]{0,1:T(8,128)(2,1)}), bf16[1600,6400]{0,1:T(8,128)(2,1)}) %all-gather.79.cloned.1.call-update) | async-done | bytes 20480016 | tf_op jit(solution)/shard_map/while/body/eval_jaxpr/all_gather | solution.py:79
  2101.4 41.5 all-gather.71.cloned.1.call-done
  2229.0 42.3 while.97
  2364.6 141.6 %all-gather.85.cloned.1.call-done = bf16[1600,4800]{0,1:T(8,128)(2,1)} async-done(((bf16[1600,600]{0,1:T(8,128)(2,1)}), bf16[1600,4800]{0,1:T(8,128)(2,1)}) %all-gather.85.cloned.1.call-update) | async-done | bytes 15360016 | tf_op jit(solution)/shard_map/while/body/eval_jaxpr/all_gather | solution.py:77
  2676.8 129.8 %all-gather.75.cloned.1.call-done = bf16[6400,1600]{0,1:T(8,128)(2,1)} async-done(((bf16[6400,200]{0,1:T(8,128)(2,1)}), bf16[6400,1600]{0,1:T(8,128)(2,1)}) %all-gather.75.cloned.1.call-update) | async-done | bytes 20480016 | tf_op jit(solution)/shard_map/while/body/eval_jaxpr/all_gather | solution.py:80
  2818.7 175.9 %all-gather.79.cloned.1.call-done = bf16[1600,6400]{0,1:T(8,128)(2,1)} async-done(((bf16[1600,800]{0,1:T(8,128)(2,1)}), bf16[1600,6400]{0,1:T(8,128)(2,1)}) %all-gather.79.cloned.1.call-update) | async-done | bytes 20480016 | tf_op jit(solution)/shard_map/while/body/eval_jaxpr/all_gather | solution.py:79
  3009.5 41.5 all-gather.71.cloned.1.call-done
  3137.1 42.3 while.97
  3273.3 141.0 %all-gather.85.cloned.1.call-done = bf16[1600,4800]{0,1:T(8,128)(2,1)} async-done(((bf16[1600,600]{0,1:T(8,128)(2,1)}), bf16[1600,4800]{0,1:T(8,128)(2,1)}) %all-gather.85.cloned.1.call-update) | async-done | bytes 15360016 | tf_op jit(solution)/shard_map/while/body/eval_jaxpr/all_gather | solution.py:77
  3558.5 334.8 %all-reduce.10.cloned.1.call-done = (bf16[1600,4800]{1,0:T(8,128)(2,1)}, bf16[1600,1600]{1,0:T(8,128)(2,1)}) async-done(((bf16[1600,4800]{1,0:T(8,128)(2,1)}, bf16[1600,1600]{1,0:T(8,128)(2,1)}), (bf16[1600,4800]{1,0:T(8,128)(2,1)}, bf16[1600,1600]{1,0:T(8,128)(2,1)})) %all-reduce.10.cloned.1.call-update) | async-done | bytes 20480016
  3900.7 198.4 %reduce-scatter.40.cloned.1.call-done = bf16[6400,200]{0,1:T(8,128)(2,1)} async-done(((bf16[6400,1600]{0,1:T(8,128)(2,1)}), bf16[6400,200]{0,1:T(8,128)(2,1)}) %reduce-scatter.40.cloned.1.call-update) | async-done | bytes 2560016
  4103.8 207.2 %reduce-scatter.32.cloned.1.call-done = bf16[800,1600]{1,0:T(8,128)(2,1)} async-done(((bf16[6400,1600]{1,0:T(8,128)(2,1)}), bf16[800,1600]{1,0:T(8,128)(2,1)}) %reduce-scatter.32.cloned.1.call-update) | async-done | bytes 2560016
  4379.8 45.9 %reduce-scatter.34.cloned.1.call-done = bf16[1600,200]{1,0:T(8,128)(2,1)} async-done(((bf16[6400,200]{1,0:T(8,128)(2,1)}), bf16[1600,200]{1,0:T(8,128)(2,1)}) %reduce-scatter.34.cloned.1.call-update) | async-done | bytes 640016
  4428.3 42.5 reduce-scatter.38.cloned.1.call-done
  (706 shorter events, 1714.5 us)
Async XLA Ops:
  63.0 272.2 %all-gather.57.cloned.1.call-start = ((), (), s32[]{:S(2)}) async-start(), calls=%async_computation.18 | async-start | bytes 3686400 | tf_op jit(solution)/shard_map/while/body/eval_jaxpr/all_gather | solution.py:208
  234.8 386.7 %all-gather.67.cloned.1.call-start = ((), (), s32[]{:S(2)}) async-start(), calls=%async_computation.23 | async-start | bytes 23961600 | tf_op jit(solution)/shard_map/while/body/eval_jaxpr/all_gather | solution.py:79
  257.2 545.7 %all-gather.63.cloned.1.call-start = ((), (), s32[]{:S(2)}) async-start(), calls=%async_computation.21 | async-start | bytes 23040000 | tf_op jit(solution)/shard_map/while/body/eval_jaxpr/all_gather | solution.py:80
  1027.2 386.2 %all-gather.67.cloned.1.call-start = ((), (), s32[]{:S(2)}) async-start(), calls=%async_computation.23 | async-start | bytes 23961600 | tf_op jit(solution)/shard_map/while/body/eval_jaxpr/all_gather | solution.py:79
  1049.2 545.4 %all-gather.63.cloned.1.call-start = ((), (), s32[]{:S(2)}) async-start(), calls=%async_computation.21 | async-start | bytes 23040000 | tf_op jit(solution)/shard_map/while/body/eval_jaxpr/all_gather | solution.py:80
  1677.7 408.6 %all-gather.79.cloned.1.call-start = ((), (), s32[]{:S(2)}) async-start(), calls=%async_computation.29 | async-start | bytes 23961600 | tf_op jit(solution)/shard_map/while/body/eval_jaxpr/all_gather | solution.py:79
  1719.9 423.0 %all-gather.71.cloned.1.call-start = ((), (), s32[]{:S(2)}) async-start(), calls=%async_computation.25 | async-start | bytes 5990400 | tf_op jit(solution)/shard_map/while/body/eval_jaxpr/all_gather | solution.py:78
  1732.3 451.6 %all-gather.69.cloned.1.call-start = ((), (), s32[]{:S(2)}) async-start(), calls=%async_computation.24 | async-start | bytes 3686400 | tf_op jit(solution)/shard_map/while/body/eval_jaxpr/all_gather | solution.py:276
  1734.2 489.8 %all-gather.81.cloned.1.call-start = ((), (), s32[]{:S(2)}) async-start(), calls=%async_computation.30 | async-start | bytes 3686400 | tf_op jit(solution)/shard_map/while/body/eval_jaxpr/all_gather | solution.py:277
  1736.1 546.3 %all-gather.83.cloned.1.call-start = ((), (), s32[]{:S(2)}) async-start(), calls=%async_computation.33 | async-start | bytes 2560000 | tf_op jit(solution)/shard_map/while/body/eval_jaxpr/all_gather | solution.py:70
  1736.7 591.7 %reduce-scatter.42.cloned.1.call-start = ((), (), s32[]{:S(2)}) async-start(), calls=%async_computation.31 | async-start | bytes 3833856 | tf_op jit(solution)/shard_map/while
  2585.9 408.6 %all-gather.79.cloned.1.call-start = ((), (), s32[]{:S(2)}) async-start(), calls=%async_computation.29 | async-start | bytes 23961600 | tf_op jit(solution)/shard_map/while/body/eval_jaxpr/all_gather | solution.py:79
  2628.2 422.8 %all-gather.71.cloned.1.call-start = ((), (), s32[]{:S(2)}) async-start(), calls=%async_computation.25 | async-start | bytes 5990400 | tf_op jit(solution)/shard_map/while/body/eval_jaxpr/all_gather | solution.py:78
  2640.6 451.6 %all-gather.69.cloned.1.call-start = ((), (), s32[]{:S(2)}) async-start(), calls=%async_computation.24 | async-start | bytes 3686400 | tf_op jit(solution)/shard_map/while/body/eval_jaxpr/all_gather | solution.py:276
  2642.5 489.7 %all-gather.81.cloned.1.call-start = ((), (), s32[]{:S(2)}) async-start(), calls=%async_computation.30 | async-start | bytes 3686400 | tf_op jit(solution)/shard_map/while/body/eval_jaxpr/all_gather | solution.py:277
  2644.4 546.2 %all-gather.83.cloned.1.call-start = ((), (), s32[]{:S(2)}) async-start(), calls=%async_computation.33 | async-start | bytes 2560000 | tf_op jit(solution)/shard_map/while/body/eval_jaxpr/all_gather | solution.py:70
  2645.0 623.0 %reduce-scatter.42.cloned.1.call-start = ((), (), s32[]{:S(2)}) async-start(), calls=%async_computation.31 | async-start | bytes 3833856 | tf_op jit(solution)/shard_map/while
  3462.5 430.9 %all-reduce.10.cloned.1.call-start = ((), (), s32[]{:S(2)}) async-start(), calls=%async_computation.14 | async-start | bytes 41779200
  3484.0 615.1 %reduce-scatter.40.cloned.1.call-start = ((), (), s32[]{:S(2)}) async-start(), calls=%async_computation.13 | async-start | bytes 23040000
  3505.3 805.7 %reduce-scatter.32.cloned.1.call-start = ((), (), s32[]{:S(2)}) async-start(), calls=%async_computation.9 | async-start | bytes 23961600
  3556.7 798.7 %reduce-scatter.30.cloned.1.call-start = ((), (), s32[]{:S(2)}) async-start(), calls=%async_computation.8 | async-start | bytes 1024000 | tf_op jit(solution)/shard_map/reduce_scatter | solution.py:378
  3895.9 481.9 %reduce-scatter.36.cloned.1.call-start = ((), (), s32[]{:S(2)}) async-start(), calls=%async_computation.11 | async-start | bytes 2560000
  3900.7 525.0 %reduce-scatter.34.cloned.1.call-start = ((), (), s32[]{:S(2)}) async-start(), calls=%async_computation.10 | async-start | bytes 4096000
  4103.8 367.1 %reduce-scatter.38.cloned.1.call-start = ((), (), s32[]{:S(2)}) async-start(), calls=%async_computation.12 | async-start | bytes 3584000
  (96 other events, 6394.6 us)
Sparse Core Ops, SparseCore 0:
  61.8 144.9 all-gather.54
  208.7 43.2 all-gather.64
  378.0 54.8 all-gather.50
  434.6 186.8 all-gather.66
  623.2 179.6 all-gather.62
  854.2 144.9 all-gather.54
  1000.9 43.1 all-gather.64
  1170.1 54.8 all-gather.50
  1226.5 186.8 all-gather.66
  1414.9 179.6 all-gather.62
  1673.2 41.5 all-gather.76
  1716.4 181.8 all-gather.74
  1899.9 186.3 all-gather.78
  2088.0 54.8 all-gather.70
  2276.9 40.7 reduce-scatter.41
  2320.1 41.1 reduce-scatter.43
  2362.9 143.2 all-gather.84
  2581.5 41.5 all-gather.76
  2624.7 181.8 all-gather.74
  2808.1 186.3 all-gather.78
  2996.2 54.8 all-gather.70
  3185.0 40.7 reduce-scatter.41
  3228.0 41.2 reduce-scatter.43
  3270.9 143.2 all-gather.84
  (16 shorter events, 603.6 us)
Sparse Core Ops, SparseCore 1:
  3484.1 409.2 all-reduce.9
  3895.6 203.5 reduce-scatter.39
  4101.4 209.6 reduce-scatter.31
  4314.6 24.7 reduce-scatter.29
  4342.5 35.2 reduce-scatter.35
  4380.8 44.9 reduce-scatter.33
  4428.6 42.2 reduce-scatter.37
where the time goes:
time: 4500 us; the launch traced here: 4480 us
  waiting for transfers between devices  3480 us (77%)
  matrix products  351 us (8%)
  local copies, waits for them, and re-layouts  275 us (6%)
  blocking collectives  200 us (4%)
  other arithmetic  122 us (3%)
    unnamed x13, waiting for transfers between devices  850 us
    all_gather x4, waiting for transfers between devices, fetch(): lax.all_gather(rows[2], 'seq', axis=1, tiled=True)  713 us
    all_gather x4, waiting for transfers between devices, fetch(): lax.all_gather(rows[3], 'seq', axis=1, tiled=True)  586 us
    all_gather x4, waiting for transfers between devices, fetch(): lax.all_gather(rows[0], 'seq', axis=1, tiled=True)  515 us
    all_gather x4, waiting for transfers between devices, fetch(): lax.all_gather(w_down, 'dp', axis=0, tiled=True)  151 us
    all_gather x4, waiting for transfers between devices, fetch(): lax.all_gather(rows[1], 'seq', axis=1, tiled=True)  148 us
    dot_general x8, matrix products, across_rows(): lax.dot_general(left, right, (((0,), (0,)), ((), ())), preferred_element_...  146 us
    all_gather x4, waiting for transfers between devices, fetch(): lax.all_gather(w_up, 'dp', axis=0, tiled=True)  108 us
  transfers between devices with their start and end apart: 47, of which 41 were waited for; matrix products, arithmetic and copies ran while one was open for 13% of the time, Pallas kernels for 0%

commit v1 on v0

v1 whole, which is shorter than its diff:
```python
import functools

import jax
import jax.numpy as jnp
from jax import lax
from jax.experimental import pallas as pl
from jax.experimental.pallas import tpu as pltpu
from jax.sharding import PartitionSpec as P

HEAD_DIM = 64
EPSILON = 1e-05
SCALE = 0.125
CUBIC = 0.044715
ROOT_TWO_PI = 0.7978845608028654
F32 = jnp.float32
BF16 = jnp.bfloat16


def dot(left, right, dims):
    return lax.dot_general(left, right, (dims, ((), ())), preferred_element_type=F32)


NN = ((1,), (0,))
NT = ((1,), (1,))
TN = ((0,), (0,))


def gelu_tanh(values):
    return (
        0.5 * values * (1.0 + jnp.tanh(ROOT_TWO_PI * (values + CUBIC * values * values * values)))
    )


def norm_forward(values, gain, shift):
    center = values - jnp.mean(values, axis=-1, keepdims=True)
    scale = lax.rsqrt(jnp.mean(center * center, axis=-1, keepdims=True) + EPSILON)
    normed = center * scale
    return (normed * gain + shift, normed, scale)


def norm_backward(grad_out, normed, scale, gain):
    scaled = grad_out * gain
    first = jnp.mean(scaled, axis=-1, keepdims=True)
    second = jnp.mean(scaled * normed, axis=-1, keepdims=True)
    return (
        scale * (scaled - first - normed * second),
        jnp.sum(grad_out * normed, axis=0),
        jnp.sum(grad_out, axis=0),
    )


def to_natural(order_ref, source, target, block):
    for slot in range(source.shape[0] // block):
        start = pl.multiple_of(order_ref[slot] * block, block)
        target[pl.ds(start, block), :] = source[slot * block : (slot + 1) * block, :]


def to_layout(order_ref, source, target, block):
    for slot in range(source.shape[0] // block):
        start = pl.multiple_of(order_ref[slot] * block, block)
        target[slot * block : (slot + 1) * block, :] = source[pl.ds(start, block), :].astype(
            target.dtype
        )


def causal(scores, tile):
    keys = lax.broadcasted_iota(jnp.int32, (tile, tile), 0)
    queries = lax.broadcasted_iota(jnp.int32, (tile, tile), 1)
    edge = jnp.where(keys <= queries, scores[-tile:, :], -1e30)
    if scores.shape[0] == tile:
        return edge
    return jnp.concatenate([scores[:-tile, :], edge], axis=0)


def attend_kernel(heads, block, tile, order_ref, joined_ref, mixed_ref, level_ref, natural, out):
    length = joined_ref.shape[0]
    span = heads * HEAD_DIM
    to_natural(order_ref, joined_ref, natural, block)
    for head in range(heads):
        low, high = head * HEAD_DIM, (head + 1) * HEAD_DIM
        values_t = natural[:, 2 * span + low : 2 * span + high].T
        for start in range(0, length, tile):
            total = start + tile
            queries = natural[start:total, low:high]
            keys = natural[:total, span + low : span + high]
            scores = causal(dot(keys, queries, NT) * SCALE, tile)
            peak = jnp.max(scores, axis=0, keepdims=True)
            raised = jnp.exp(scores - peak)
            summed = jnp.sum(raised, axis=0, keepdims=True)
            weights = (raised * (1.0 / summed)).astype(BF16)
            part = dot(values_t[:, :total], weights, NN)
            out[start:total, low:high] = part.T
            level_ref[head : head + 1, start:total] = peak + jnp.log(summed)
    to_layout(order_ref, out, mixed_ref, block)


def attend_back_kernel(
    heads, block, tile, order_ref, joined_ref, grad_ref, level_ref, result_ref,
    natural, grads, out, keys_sum, values_sum,
):
    length = joined_ref.shape[0]
    span = heads * HEAD_DIM
    to_natural(order_ref, joined_ref, natural, block)
    to_natural(order_ref, grad_ref, grads, block)
    for head in range(heads):
        low, high = head * HEAD_DIM, (head + 1) * HEAD_DIM
        keys_all = natural[:, span + low : span + high]
        values_all = natural[:, 2 * span + low : 2 * span + high]
        keys_t = keys_all.T
        for start in reversed(range(0, length, tile)):
            total = start + tile
            queries = natural[start:total, low:high]
            grad_part = grads[start:total, low:high]
            scores = causal(dot(keys_all[:total], queries, NT) * SCALE, tile)
            weights = jnp.exp(scores - level_ref[head : head + 1, start:total])
            grad_weights = dot(values_all[:total], grad_part, NT)
            offset = jnp.sum(weights * grad_weights, axis=0, keepdims=True)
            grad_scores = (weights * (grad_weights - offset)).astype(BF16)
            values_term = dot(weights.astype(BF16), grad_part, NN)
            keys_term = dot(grad_scores, queries, NN)
            query_term = dot(keys_t[:, :total], grad_scores, NN)
            out[start:total, low:high] = query_term.T * SCALE
            if total == length:
                keys_sum[...] = keys_term
                values_sum[...] = values_term
            else:
                keys_sum[:total, :] += keys_term
                values_sum[:total, :] += values_term
        out[:, span + low : span + high] = keys_sum[...] * SCALE
        out[:, 2 * span + low : 2 * span + high] = values_sum[...]
    to_layout(order_ref, out, result_ref, block)


VMEM_SPEC = pl.BlockSpec(memory_space=pltpu.VMEM)
SMEM_SPEC = pl.BlockSpec(memory_space=pltpu.SMEM)


def attend(order, joined, heads, block):
    length, span = joined.shape[0], heads * HEAD_DIM
    tile = min(256, length)
    pairs = heads * length * (length + tile) // 2
    return pl.pallas_call(
        functools.partial(attend_kernel, heads, block, tile),
        out_shape=(
            jax.ShapeDtypeStruct((length, span), BF16),
            jax.ShapeDtypeStruct((heads, length), F32),
        ),
        in_specs=[SMEM_SPEC, VMEM_SPEC],
        out_specs=(VMEM_SPEC, VMEM_SPEC),
        scratch_shapes=[pltpu.VMEM((length, 3 * span), BF16), pltpu.VMEM((length, span), F32)],
        cost_estimate=pl.CostEstimate(
            flops=pairs * 256, transcendentals=pairs, bytes_accessed=length * span * 8
        ),
        name="attend",
    )(order, joined)


def attend_back(order, joined, grad_mixed, level, heads, block):
    length, span = joined.shape[0], heads * HEAD_DIM
    tile = min(256, length)
    pairs = heads * length * (length + tile) // 2
    return pl.pallas_call(
        functools.partial(attend_back_kernel, heads, block, tile),
        out_shape=jax.ShapeDtypeStruct((length, 3 * span), BF16),
        in_specs=[SMEM_SPEC, VMEM_SPEC, VMEM_SPEC, VMEM_SPEC],
        out_specs=VMEM_SPEC,
        scratch_shapes=[
            pltpu.VMEM((length, 3 * span), BF16),
            pltpu.VMEM((length, span), BF16),
            pltpu.VMEM((length, 3 * span), F32),
            pltpu.VMEM((length, HEAD_DIM), F32),
            pltpu.VMEM((length, HEAD_DIM), F32),
        ],
        cost_estimate=pl.CostEstimate(
            flops=pairs * 640, transcendentals=pairs, bytes_accessed=length * span * 14
        ),
        name="attend_back",
    )(order, joined, grad_mixed, level)


def shards(layer_input, cotangent, block_order, w_qkv, w_out, w_up, w_down, vectors):
    n_dp, n_seq = lax.axis_size("dp"), lax.axis_size("seq")
    dp, seq = lax.axis_index("dp"), lax.axis_index("seq")
    micro, local, per, width = layer_input.shape
    block = per // 2
    length = per * n_seq
    tokens = micro * local * per
    sequences = n_dp * micro * local
    ff_local = w_up.shape[1]
    ff_piece = ff_local // n_dp
    d_row, d_col = w_qkv.shape[0], w_out.shape[1]
    heads_all = width // HEAD_DIM
    groups = n_seq // sequences
    heads = -(-heads_all // (n_dp * groups))
    padded = n_dp * groups * heads
    span = heads * HEAD_DIM
    wide = groups * 3 * span

    def gather(x, axis, dim=0):
        return lax.all_gather(x, axis, axis=dim, tiled=True)

    def scatter(x, axis, dim=0):
        return lax.psum_scatter(x.astype(BF16), axis, scatter_dimension=dim, tiled=True)

    def swap(x, axis):
        return lax.all_to_all(x, axis, 0, 0, tiled=True)

    small = gather(gather(vectors, "dp"), "seq", 1)
    table = small.astype(F32)

    qkv_rows = gather(w_qkv[None], "seq")
    qkv_rows = qkv_rows.transpose(1, 0, 2).reshape(d_row, 3, heads_all, HEAD_DIM)
    qkv_rows = jnp.pad(qkv_rows, ((0, 0), (0, 0), (0, padded - heads_all), (0, 0)))
    qkv_rows = qkv_rows.reshape(d_row, 3, n_dp, groups, span).transpose(2, 0, 3, 1, 4)
    qkv = swap(qkv_rows.reshape(n_dp, d_row, wide), "dp").reshape(width, wide)

    up_send = w_up.T.reshape(n_dp, ff_piece, d_row)
    down_send = w_down.T.reshape(d_col, n_seq // n_dp, n_dp, ff_piece).transpose(2, 0, 1, 3)
    down_send = down_send.reshape(n_dp, d_col, -1)
    up_part = swap(up_send, "dp").transpose(1, 0, 2).reshape(ff_piece, width)
    down_part = swap(down_send, "dp").transpose(1, 0, 2).reshape(d_col, -1)
    up_t = gather(up_part, "seq")
    down_t = gather(down_part, "seq")

    out_t = gather(gather(w_out.T, "seq")[None], "dp").transpose(1, 0, 2).reshape(width, width)

    def bias_heads(rows):
        rows = jnp.pad(rows.reshape(heads_all, HEAD_DIM), ((0, padded - heads_all), (0, 0)))
        rows = rows.reshape(n_dp, groups, span)
        return lax.dynamic_index_in_dim(rows, dp, 0, keepdims=False)

    nothing = jnp.zeros((groups, span), F32)
    qkv_bias = jnp.stack([bias_heads(table[4]), nothing, bias_heads(table[5])], axis=1)
    qkv_bias = qkv_bias.reshape(1, wide)
    up_bias = table[8:].reshape(n_seq, n_dp, ff_piece)
    up_bias = lax.dynamic_index_in_dim(up_bias, dp, 1, keepdims=False).reshape(1, -1)

    def to_sequences(x):
        columns = x.shape[-1] // groups
        x = x.reshape(sequences, per, groups, columns).transpose(0, 2, 1, 3)
        return swap(x.reshape(n_seq, per, columns), "seq").reshape(length, columns)

    def to_tokens(x):
        columns = x.shape[-1]
        x = swap(x.reshape(n_seq, per, columns), "seq")
        x = x.reshape(sequences, groups, per, columns).transpose(0, 2, 1, 3)
        return x.reshape(n_dp * tokens, groups * columns)

    residual = layer_input.reshape(tokens, width).astype(F32)
    cot = cotangent.reshape(tokens, width)
    entry_one, first_norm, first_scale = norm_forward(residual, table[0], table[1])
    entries_one = gather(entry_one.astype(BF16), "dp")
    cots = gather(cot, "dp")
    joined = (dot(entries_one, qkv, NN) + qkv_bias).astype(BF16)
    joined = to_sequences(joined)
    mixed, level = attend(block_order, joined, heads, block)

    mixed = swap(to_tokens(mixed).reshape(n_dp, tokens, groups * span), "dp")
    mixed = mixed.transpose(1, 0, 2).reshape(tokens, padded * HEAD_DIM)[:, :width]
    middle = residual + dot(mixed, out_t, NT) + table[6]
    entry_two, second_norm, second_scale = norm_forward(middle, table[2], table[3])
    entries_two = gather(entry_two.astype(BF16), "dp")
    hidden_pre = dot(entries_two, up_t, NT) + up_bias
    hidden = gelu_tanh(hidden_pre).astype(BF16)
    branch = scatter(dot(hidden, down_t, NT), "dp").astype(F32)
    output = (middle + branch + table[7]).astype(BF16)

    cot_wide = cot.astype(F32)
    grad_hidden = dot(cots, down_t, NN)
    ignored, pull = jax.vjp(gelu_tanh, hidden_pre)
    grad_pre = pull(grad_hidden)[0].astype(BF16)
    grad_entry_two = scatter(dot(grad_pre, up_t, NN), "dp").astype(F32)
    grad_down_t = scatter(dot(cots, hidden, TN), "seq")
    grad_up_t = scatter(dot(grad_pre, entries_two, TN), "seq")
    grad_middle, grad_gain_two, grad_shift_two = norm_backward(
        grad_entry_two, second_norm, second_scale, table[2]
    )
    grad_middle = grad_middle + cot_wide
    grad_branch = grad_middle.astype(BF16)
    grad_mixed = dot(grad_branch, out_t, NN).astype(BF16)
    grad_mixed = jnp.pad(grad_mixed, ((0, 0), (0, padded * HEAD_DIM - width)))
    grad_mixed = grad_mixed.reshape(tokens, n_dp, groups * span).transpose(1, 0, 2)
    grad_mixed = to_sequences(swap(grad_mixed, "dp"))
    grad_out = scatter(scatter(dot(mixed, grad_branch, TN), "dp").T, "seq")

    grad_joined = attend_back(block_order, joined, grad_mixed, level, heads, block)
    grad_joined = to_tokens(grad_joined)
    grad_entry_one = scatter(dot(grad_joined, qkv, NT), "dp").astype(F32)
    grad_qkv = dot(entries_one, grad_joined, TN).astype(BF16)
    grad_qkv = swap(grad_qkv.reshape(n_dp, d_row, wide), "dp")
    grad_qkv = grad_qkv.reshape(n_dp, d_row, groups, 3, span).transpose(1, 3, 0, 2, 4)
    grad_qkv = grad_qkv.reshape(d_row, 3, padded * HEAD_DIM)[:, :, :width]
    grad_qkv = grad_qkv.reshape(d_row, n_seq, -1).transpose(1, 0, 2)
    grad_qkv = scatter(grad_qkv, "seq").reshape(d_row, -1)

    grad_residual, grad_gain_one, grad_shift_one = norm_backward(
        grad_entry_one, first_norm, first_scale, table[0]
    )
    grad_input = (grad_residual + grad_middle).astype(BF16)

    grad_up = swap(grad_up_t.reshape(ff_piece, n_dp, d_row).transpose(1, 0, 2), "dp")
    grad_up = grad_up.reshape(ff_local, d_row).T
    grad_down = swap(grad_down_t.reshape(d_col, n_dp, -1).transpose(1, 0, 2), "dp")
    grad_down = grad_down.reshape(n_dp, d_col, n_seq // n_dp, ff_piece).transpose(2, 0, 3, 1)
    grad_down = grad_down.reshape(w_down.shape)

    own = (jnp.arange(n_dp) == dp).astype(F32)
    joined_sum = jnp.sum(grad_joined.astype(F32), axis=0).reshape(1, groups, 3, span)
    joined_sum = (own[:, None, None, None] * joined_sum).transpose(2, 0, 1, 3)
    joined_sum = joined_sum.reshape(3, padded * HEAD_DIM)[:, :width]
    up_sum = jnp.sum(grad_pre.astype(F32), axis=0).reshape(n_seq, 1, ff_piece)
    up_sum = (own[None, :, None] * up_sum).reshape(-1, width)
    rows = jnp.stack(
        [
            grad_gain_one,
            grad_shift_one,
            grad_gain_two,
            grad_shift_two,
            joined_sum[0],
            joined_sum[2],
            jnp.sum(grad_branch.astype(F32), axis=0),
            jnp.sum(cot_wide, axis=0),
        ]
    )
    rows = lax.psum(jnp.concatenate([rows, up_sum], axis=0), ("dp", "seq"))
    grad_vectors = lax.dynamic_slice(
        rows, (dp * vectors.shape[0], seq * vectors.shape[1]), vectors.shape
    )
    return (
        output.reshape(layer_input.shape),
        grad_input.reshape(layer_input.shape),
        grad_qkv.astype(F32),
        grad_out.T.astype(F32),
        grad_up.astype(F32),
        grad_down.astype(F32),
        grad_vectors,
    )


def solution(mesh):
    both = P(None, "dp", "seq", None)
    matrix = P("dp", "seq")
    return jax.shard_map(
        shards,
        mesh=mesh,
        in_specs=(both, both, P(), matrix, matrix, matrix, matrix, matrix),
        out_specs=(both, both, matrix, matrix, matrix, matrix, matrix),
        check_vma=False,
    )
```

time: 4500 us -> 1310 us (0.29)
  waiting for transfers between devices: 3480 us -> 712 us
  matrix products: 351 us -> 112 us
  local copies, waits for them, and re-layouts: 275 us -> 169 us
  other arithmetic: 122 us -> 22.5 us
    all_gather x36 -> x8, waiting for transfers between devices: 2590 us -> 140 us  [gather(): return lax.all_gather(x, axis, axis=dim, tiled=True)]
    unnamed x13 -> x21, waiting for transfers between devices: 850 us -> 93.1 us
    dot_general x94 -> x12, matrix products: 351 us -> 112 us  [dot(): lax.dot_general(left, right, (dims, ((), ())), preferred_element_type=F32)]
    all_to_all x0 -> x7, waiting for transfers between devices: none -> 224 us  [swap(): return lax.all_to_all(x, axis, 0, 0, tiled=True)]
    all_to_all x0 -> x5, blocking collectives: none -> 169 us  [swap(): return lax.all_to_all(x, axis, 0, 0, tiled=True)]
    all_gather x12 -> x2, blocking collectives: 163 us -> 24.1 us  [gather(): return lax.all_gather(x, axis, axis=dim, tiled=True)]
    reduce_scatter x1 -> x4, waiting for transfers between devices: 0.01 us -> 136 us  [scatter(): lax.psum_scatter(x.astype(BF16), axis, scatter_dimension=dim, tiled=True)]
    psum x0 -> x1, waiting for transfers between devices: none -> 119 us  [shards(): rows = lax.psum(jnp.concatenate([rows, up_sum], axis=0), ('dp', 'seq'))]
  transfers between devices with their start and end apart: 47 -> 24, of which waited for: 41 -> 16; matrix products, arithmetic and copies ran while one was open for 13% -> 20% of each run, Pallas kernels for 0% -> 3%
where the time goes in v1:
time: 1310 us; the launch traced here: 1290 us
  waiting for transfers between devices  712 us (54%)
  blocking collectives  193 us (15%)
  local copies, waits for them, and re-layouts  169 us (13%)
  matrix products  112 us (9%)
  Pallas kernels  37.5 us (3%)
  starting transfers between devices  31.2 us (2%)
  other arithmetic  22.5 us (2%)
  between operations  15.6 us (1%)
    all_to_all x7, waiting for transfers between devices, swap(): return lax.all_to_all(x, axis, 0, 0, tiled=True)  224 us
    all_to_all x5, blocking collectives, swap(): return lax.all_to_all(x, axis, 0, 0, tiled=True)  169 us
    all_gather x8, waiting for transfers between devices, gather(): return lax.all_gather(x, axis, axis=dim, tiled=True)  140 us
    reduce_scatter x4, waiting for transfers between devices, scatter(): lax.psum_scatter(x.astype(BF16), axis, scatter_dimension=dim, tiled=True)  136 us
    psum x1, waiting for transfers between devices, shards(): rows = lax.psum(jnp.concatenate([rows, up_sum], axis=0), ('dp', 'seq'))  119 us
    dot_general x12, matrix products, dot(): lax.dot_general(left, right, (dims, ((), ())), preferred_element_type=F32)  112 us
    unnamed x21, waiting for transfers between devices  93.1 us
    unnamed x46, local copies, waits for them, and re-layouts  33.3 us
  transfers between devices with their start and end apart: 24, of which 16 were waited for; matrix products, arithmetic and copies ran while one was open for 20% of the time, Pallas kernels for 3%

profile of v1, /device:TPU:0, one launch (start us, length us, event | category | flops | bytes accessed | tf_op | source)
XLA Modules:
  0.0 1293.0 jit_solution(14775193922749880281)
XLA Ops:
  19.6 14.4 %all-gather.3 = bf16[8,200,12]{1,2,0:T(8,128)(2,1)S(1)} all-gather(bf16[1,200,12]{1,2,0:T(8,128)(2,1)S(1)} %bitcast.192), channel_id=1, replica_groups=mesh['dp'=4,'seq'=8] {'seq'}, dimensions={0}, use_global_device_ids=true | all-gather | bytes 43200 | tf_op jit(solution)/shard_map/all_gather | solution.py:200
  46.4 39.5 %all-gather.26.cloned.1.call-done = bf16[3200,600]{1,0:T(8,128)(2,1)} async-done(((bf16[400,600]{1,0:T(8,128)(2,1)}), bf16[3200,600]{1,0:T(8,128)(2,1)}) %all-gather.26.cloned.1.call-update) | async-done | bytes 3840016 | tf_op jit(solution)/shard_map/all_gather | solution.py:200
  114.7 65.4 %all-to-all-done = bf16[4,400,1344]{2,1,0:T(8,128)(2,1)} async-done(((bf16[4,400,1344]{2,1,0:T(8,128)(2,1)}), bf16[4,400,1344]{2,1,0:T(8,128)(2,1)}, u32[]{:S(2)}, u32[]{:S(2)}) %all-to-all-start) | async-done | bytes 4300832 | tf_op jit(solution)/shard_map/all_to_all | solution.py:206
  211.1 96.7 %all-to-all-done.1 = bf16[8,128,1344]{1,2,0:T(8,128)(2,1)} async-done(((bf16[8,128,1344]{1,2,0:T(8,128)(2,1)}), bf16[8,128,1344]{1,2,0:T(8,128)(2,1)}, u32[]{:S(2)}, u32[]{:S(2)}) %all-to-all-start.1) | async-done | bytes 2752544 | tf_op jit(solution)/shard_map/all_to_all | solution.py:206
  312.6 16.7 %attend.1 = (bf16[1024,448]{1,0:T(8,128)(2,1)}, f32[7,1024]{1,0:T(8,128)}) custom-call(s32[16]{0:T(128)} %order_ref.3, bf16[1024,1344]{1,0:T(8,128)(2,1)} %bitcast.179), custom_call_target="tpu_custom_call" | custom-call | flops 1174405120 | bytes 3670016 | tf_op jit(solution)/shard_map/attend/pallas_call | solution.py:142
  330.9 26.6 %all_to_all.60 = bf16[8,128,448]{1,2,0:T(8,128)(2,1)S(1)} all-to-all(bf16[8,128,448]{1,2,0:T(8,128)(2,1)S(1)} %copy.161), channel_id=1, replica_groups=mesh['dp'=4,'seq'=8] {'seq'}, dimensions={0} | all-to-all | bytes 1835008 | tf_op jit(solution)/shard_map/all_to_all | solution.py:206
  363.3 12.2 all-to-all-done.3
  398.6 22.0 %all_to_all.61 = bf16[4,200,400]{1,2,0:T(8,128)(2,1)} all-to-all(bf16[4,200,400]{1,2,0:T(8,128)(2,1)} %bitcast.176), channel_id=1, replica_groups=mesh['dp'=4,'seq'=8] {'dp'}, dimensions={0} | all-to-all | bytes 1280000 | tf_op jit(solution)/shard_map/all_to_all | solution.py:206
  442.3 34.7 %all-gather.24.cloned.1.call-done = bf16[1024,1600]{0,1:T(8,128)(2,1)} async-done(((bf16[256,1600]{0,1:T(8,128)(2,1)}), bf16[1024,1600]{0,1:T(8,128)(2,1)}) %all-gather.24.cloned.1.call-update) | async-done | bytes 3276816 | tf_op jit(solution)/shard_map/all_gather | solution.py:200
  477.0 58.9 %all-gather.22.cloned.1.call-done = bf16[1600,1600]{1,0:T(8,128)(2,1)} async-done(((bf16[200,1600]{1,0:T(8,128)(2,1)}), bf16[1600,1600]{1,0:T(8,128)(2,1)}) %all-gather.22.cloned.1.call-update) | async-done | bytes 5120016 | tf_op jit(solution)/shard_map/all_gather | solution.py:200
  535.9 16.2 %convert_reduce_fusion = (f32[1600]{0:T(1024)S(1)}, bf16[1024,1600]{0,1:T(8,128)(2,1)S(1)}) fusion(f32[1024,1600]{0,1:T(8,128)} %fusion.40, f32[1600]{0:T(1024)S(1)} %add.153, bf16[1024,1600]{0,1:T(8,128)(2,1)} %all-gather.24.cloned.1.call-done, bf16[1600,1600]{1,0:T(8,128)(2,1)} %all-gather.22.cloned.1.call-done), kind=kOutput, calls=%fused_computation.14 | convolution fusion | flops 5287115264 | bytes 18240000 | tf_op jit(solution)/shard_map/dot_general | solution.py:20
  564.3 11.5 convolution_convert_fusion.5
  575.9 32.0 %reduce-scatter.17.cloned.1.call-done = bf16[256,1600]{0,1:T(8,128)(2,1)} async-done(((bf16[1024,1600]{0,1:T(8,128)(2,1)}), bf16[256,1600]{0,1:T(8,128)(2,1)}) %reduce-scatter.17.cloned.1.call-update) | async-done | bytes 819216 | tf_op jit(solution)/shard_map/reduce_scatter | solution.py:203
  610.1 45.8 %reduce-scatter.15.cloned.1.call-done = bf16[256,1600]{0,1:T(8,128)(2,1)} async-done(((bf16[1024,1600]{0,1:T(8,128)(2,1)}), bf16[256,1600]{0,1:T(8,128)(2,1)}) %reduce-scatter.15.cloned.1.call-update) | async-done | bytes 819216 | tf_op jit(solution)/shard_map/reduce_scatter | solution.py:203
  670.1 25.5 %all_to_all.62 = bf16[4,256,448]{1,2,0:T(8,128)(2,1)S(1)} all-to-all(bf16[4,256,448]{1,2,0:T(8,128)(2,1)S(1)} %bitcast.171), channel_id=1, replica_groups=mesh['dp'=4,'seq'=8] {'dp'}, dimensions={0} | all-to-all | bytes 1835008 | tf_op jit(solution)/shard_map/all_to_all | solution.py:206
  701.1 28.3 %all_to_all.63 = bf16[8,128,448]{1,2,0:T(8,128)(2,1)} all-to-all(bf16[8,128,448]{1,2,0:T(8,128)(2,1)S(1)} %copy.172), channel_id=1, replica_groups=mesh['dp'=4,'seq'=8] {'seq'}, dimensions={0} | all-to-all | bytes 1835008 | tf_op jit(solution)/shard_map/all_to_all | solution.py:206
  732.0 20.8 %attend_back.1 = bf16[1024,1344]{1,0:T(8,128)(2,1)} custom-call(s32[16]{0:T(128)} %order_ref.3, bf16[1024,1344]{1,0:T(8,128)(2,1)} %bitcast.180, bf16[1024,448]{1,0:T(8,128)(2,1)} %bitcast.185, f32[7,1024]{1,0:T(8,128)} %get-tuple-element.10.level_ref), custom_call_target="tpu_custom_call" | custom-call | flops 2936012800 | bytes 6422528 | tf_op jit(solution)/shard_map/attend_back/pallas_call | solution.py:162
  757.4 66.6 %all_to_all.64 = bf16[8,128,1344]{1,2,0:T(8,128)(2,1)S(1)} all-to-all(bf16[8,128,1344]{1,2,0:T(8,128)(2,1)} %copy.174), channel_id=1, replica_groups=mesh['dp'=4,'seq'=8] {'seq'}, dimensions={0} | all-to-all | bytes 5505024 | tf_op jit(solution)/shard_map/all_to_all | solution.py:206
  834.5 12.3 fusion.6
  890.8 39.0 %all-to-all-done.9 = bf16[4,400,1344]{2,1,0:T(8,128)(2,1)} async-done(((bf16[4,400,1344]{2,1,0:T(8,128)(2,1)}), bf16[4,400,1344]{2,1,0:T(8,128)(2,1)}, u32[]{:S(2)}, u32[]{:S(2)}) %all-to-all-start.9) | async-done | bytes 4300832 | tf_op jit(solution)/shard_map/all_to_all | solution.py:206
  971.5 27.0 %all-reduce.12.cloned.1.call-done = bf16[1600,1600]{0,1:T(8,128)(2,1)} async-done(((bf16[1600,1600]{0,1:T(8,128)(2,1)}), bf16[1600,1600]{0,1:T(8,128)(2,1)}) %all-reduce.12.cloned.1.call-update) | async-done | bytes 5120016
  1005.2 56.4 %reduce-scatter.27.cloned.1.call-done = bf16[200,1600]{1,0:T(8,128)(2,1)} async-done(((bf16[1600,1600]{1,0:T(8,128)(2,1)}), bf16[200,1600]{1,0:T(8,128)(2,1)}) %reduce-scatter.27.cloned.1.call-update) | async-done | bytes 640016
  1104.8 118.8 %all-reduce.10.cloned.1.call-done = f32[12,1600]{1,0:T(8,128)} async-done(((f32[12,1600]{1,0:T(8,128)}), f32[12,1600]{1,0:T(8,128)}) %all-reduce.10.cloned.1.call-update) | async-done | bytes 76816 | tf_op jit(solution)/shard_map/psum | solution.py:325
  1225.0 58.4 %reduce-scatter.21.cloned.1.call-done = bf16[1,400,600]{1,2,0:T(8,128)(2,1)} async-done(((bf16[8,400,600]{1,2,0:T(8,128)(2,1)}), bf16[1,400,600]{1,2,0:T(8,128)(2,1)}) %reduce-scatter.21.cloned.1.call-update) | async-done | bytes 480016 | tf_op jit(solution)/shard_map/reduce_scatter | solution.py:203
  (199 shorter events, 331.5 us)
Async XLA Ops:
  7.2 35.7 %all-gather.16.cloned.1.call-start = ((), (), s32[]{:S(2)}) async-start(), calls=%async_computation.20 | async-start | bytes 1843200 | tf_op jit(solution)/shard_map/all_gather | solution.py:200
  9.0 76.9 %all-gather.26.cloned.1.call-start = ((), (), s32[]{:S(2)}) async-start(), calls=%async_computation.30 | async-start | bytes 4608000 | tf_op jit(solution)/shard_map/all_gather | solution.py:200
  9.8 173.9 %all-gather.14.cloned.1.call-start = ((), (), s32[]{:S(2)}) async-start(), calls=%async_computation.19 | async-start | bytes 4096000 | tf_op jit(solution)/shard_map/all_gather | solution.py:200
  42.8 320.5 %all-gather.28.cloned.1.call-start = ((), (), s32[]{:S(2)}) async-start(), calls=%async_computation.31 | async-start | bytes 6656000 | tf_op jit(solution)/shard_map/all_gather | solution.py:200
  107.9 72.3 %all-to-all-start = ((bf16[4,400,1344]{2,1,0:T(8,128)(2,1)}), bf16[4,400,1344]{2,1,0:T(8,128)(2,1)}, u32[]{:S(2)}, u32[]{:S(2)}) async-start(bf16[4,400,1344]{2,1,0:T(8,128)(2,1)} %copy.158), calls=%async_computation | async-start | bytes 9011200 | tf_op jit(solution)/shard_map/all_to_all | solution.py:206
  180.1 24.5 %all-to-all-start.4 = ((bf16[4,200,400]{2,1,0:T(8,128)(2,1)}), bf16[4,200,400]{2,1,0:T(8,128)(2,1)S(1)}, u32[]{:S(2)}, u32[]{:S(2)}) async-start(bf16[4,200,400]{2,1,0:T(8,128)(2,1)} %bitcast.22), calls=%async_computation.4 | async-start | bytes 1638400 | tf_op jit(solution)/shard_map/all_to_all | solution.py:206
  204.6 103.2 %all-to-all-start.1 = ((bf16[8,128,1344]{1,2,0:T(8,128)(2,1)}), bf16[8,128,1344]{1,2,0:T(8,128)(2,1)}, u32[]{:S(2)}, u32[]{:S(2)}) async-start(bf16[8,128,1344]{1,2,0:T(8,128)(2,1)} %bitcast.164), calls=%async_computation.1 | async-start | bytes 5505024 | tf_op jit(solution)/shard_map/all_to_all | solution.py:206
  209.0 215.1 %all-gather.20.cloned.1.call-start = ((), (), s32[]{:S(2)}) async-start(), calls=%async_computation.22 | async-start | bytes 5990400 | tf_op jit(solution)/shard_map/all_gather | solution.py:200
  359.7 15.8 %all-to-all-start.3 = ((bf16[4,256,448]{1,2,0:T(8,128)(2,1)}), bf16[4,256,448]{1,2,0:T(8,128)(2,1)S(1)}, u32[]{:S(2)}, u32[]{:S(2)}) async-start(bf16[4,256,448]{1,2,0:T(8,128)(2,1)} %copy.163), calls=%async_computation.3 | async-start | bytes 1835008 | tf_op jit(solution)/shard_map/all_to_all | solution.py:206
  363.2 68.0 %all-gather.18.cloned.1.call-start = ((), (), s32[]{:S(2)}) async-start(), calls=%async_computation.21 | async-start | bytes 4096000 | tf_op jit(solution)/shard_map/all_gather | solution.py:200
  383.3 93.7 %all-gather.24.cloned.1.call-start = ((), (), s32[]{:S(2)}) async-start(), calls=%async_computation.25 | async-start | bytes 4096000 | tf_op jit(solution)/shard_map/all_gather | solution.py:200
  391.8 144.1 %all-gather.22.cloned.1.call-start = ((), (), s32[]{:S(2)}) async-start(), calls=%async_computation.23 | async-start | bytes 5990400 | tf_op jit(solution)/shard_map/all_gather | solution.py:200
  422.9 185.1 %reduce-scatter.17.cloned.1.call-start = ((), (), s32[]{:S(2)}) async-start(), calls=%async_computation.26 | async-start | bytes 4096000 | tf_op jit(solution)/shard_map/reduce_scatter | solution.py:203
  564.1 91.8 %reduce-scatter.15.cloned.1.call-start = ((), (), s32[]{:S(2)}) async-start(), calls=%async_computation.24 | async-start | bytes 4096000 | tf_op jit(solution)/shard_map/reduce_scatter | solution.py:203
  575.9 303.0 %reduce-scatter.25.cloned.1.call-start = ((), (), s32[]{:S(2)}) async-start(), calls=%async_computation.34 | async-start | bytes 6656000
  664.5 222.8 %reduce-scatter.19.cloned.1.call-start = ((), (), s32[]{:S(2)}) async-start(), calls=%async_computation.27 | async-start | bytes 4096000 | tf_op jit(solution)/shard_map/reduce_scatter | solution.py:203
  834.5 164.0 %all-reduce.12.cloned.1.call-start = ((), (), s32[]{:S(2)}) async-start(), calls=%async_computation.33 | async-start | bytes 10649600
  846.9 214.7 %reduce-scatter.27.cloned.1.call-start = ((), (), s32[]{:S(2)}) async-start(), calls=%async_computation.35 | async-start | bytes 5990400
  873.9 55.9 %all-to-all-start.9 = ((bf16[4,400,1344]{2,1,0:T(8,128)(2,1)}), bf16[4,400,1344]{2,1,0:T(8,128)(2,1)}, u32[]{:S(2)}, u32[]{:S(2)}) async-start(bf16[4,400,1344]{2,1,0:T(8,128)(2,1)} %bitcast.163), calls=%async_computation.12 | async-start | bytes 9011200 | tf_op jit(solution)/shard_map/all_to_all | solution.py:206
  878.9 218.4 %reduce-scatter.23.cloned.1.call-start = ((), (), s32[]{:S(2)}) async-start(), calls=%async_computation.32 | async-start | bytes 1843200
  882.4 341.2 %all-reduce.10.cloned.1.call-start = ((), (), s32[]{:S(2)}) async-start(), calls=%async_computation.29 | async-start | bytes 212992 | tf_op jit(solution)/shard_map/psum | solution.py:325
  890.8 392.7 %reduce-scatter.21.cloned.1.call-start = ((), (), s32[]{:S(2)}) async-start(), calls=%async_computation.28 | async-start | bytes 5529600 | tf_op jit(solution)/shard_map/reduce_scatter | solution.py:203
  1001.0 66.6 %all-to-all-start.11 = ((bf16[4,200,400]{1,2,0:T(8,128)(2,1)}), bf16[4,200,400]{1,2,0:T(8,128)(2,1)}, u32[]{:S(2)}, u32[]{:S(2)}) async-start(bf16[4,200,400]{1,2,0:T(8,128)(2,1)} %bitcast.175), calls=%async_computation.15 | async-start | bytes 1638400 | tf_op jit(solution)/shard_map/all_to_all | solution.py:206
  1067.6 15.3 %all-to-all-start.10 = ((bf16[4,200,400]{2,1,0:T(8,128)(2,1)}), bf16[4,200,400]{2,1,0:T(8,128)(2,1)}, u32[]{:S(2)}, u32[]{:S(2)}) async-start(bf16[4,200,400]{2,1,0:T(8,128)(2,1)} %bitcast.172), calls=%async_computation.14 | async-start | bytes 1638400 | tf_op jit(solution)/shard_map/all_to_all | solution.py:206
  (17 other events, 86.6 us)
Sparse Core Ops, SparseCore 0:
  10.2 28.6 all-gather.15
  40.5 45.3 all-gather.25
  88.3 83.6 all-gather.13
  174.3 70.5 all-gather.27
  246.4 70.0 all-gather.19
  383.4 47.7 all-gather.17
  433.6 43.3 all-gather.23
  479.2 56.6 all-gather.21
  564.2 43.7 reduce-scatter.16
  610.8 44.9 reduce-scatter.14
  664.6 73.2 reduce-scatter.24
  834.6 42.9 reduce-scatter.18
  880.0 118.4 all-reduce.11
  1000.7 60.8 reduce-scatter.26
  1063.7 33.5 reduce-scatter.22
  1102.7 120.8 all-reduce.9
  1225.7 57.6 reduce-scatter.20
